TPU v7x, 256 devices: a whole 4x4x8 slice. The times are simulated.
256 devices in a mesh: dp: 8 (over z), w: 4 (over y), h: 8 (over x, core).
Axes of the slice: x: 4, y: 4, z: 8, core: 2. Of those that a mesh axis runs over, the one named last changes fastest.
Arguments:
- field: float32 [96, 32, 128, 256], P('dp', None, 'h', 'w')
- target: float32 [96, 32, 128, 256], P('dp', None, 'h', 'w')
- lat_weight: float32 [128], P('h')
- leg_fwd: float32 [64, 64, 128], P('w', None, 'h')
- leg_inv: float32 [64, 64, 128], P('w', None, 'h')
- spec_w: float32 [2, 64, 32, 32], replicated
- w_in: bfloat16 [32, 64], replicated
- w_out: bfloat16 [64, 32], replicated
Outputs:
- output 1: float32 [], replicated
- output 2: float32 [96, 32, 128, 256], P('dp', None, 'h', 'w')
- output 3: float32 [2, 64, 32, 32], P(None, 'h')
- output 4: float32 [32, 64], replicated
- output 5: float32 [64, 32], replicated
All inputs are finite; a program needn't handle non-finite values.
Results may differ from a plain program's by a relative error of at most 0.00127219.
Values sent between devices are 32-bit elements.
A program may use at most 768 MiB of HBM per device.

v0:
```python
import functools
import jax
import jax.numpy as jnp
from jax import lax
from jax.sharding import PartitionSpec as P

NORM_EPS = 1e-5
PRECISE = lax.Precision.HIGHEST


def precise_product(einsum_form, operand_a, operand_b):
    return jnp.einsum(einsum_form, operand_a, operand_b, precision=PRECISE, preferred_element_type=jnp.float32)


def lon_forward(grid_vals, num_modes):
    lon_spec = jnp.fft.rfft(grid_vals, axis=3, norm="ortho")[:, :, :, :num_modes]
    return jnp.stack([lon_spec.real, lon_spec.imag])


def lon_inverse(coeffs, lon_count):
    pad_width = ((0, 0), (0, 0), (0, 0), (0, lon_count // 2 + 1 - coeffs.shape[4]))
    padded = jnp.pad(lax.complex(coeffs[0], coeffs[1]), pad_width)
    return jnp.fft.irfft(padded, n=lon_count, axis=3, norm="ortho")


def spectral_mix(coeffs, kernel):
    einsum_form = "bilm,lio->bolm"
    real_part = precise_product(einsum_form, coeffs[0], kernel[0]) - precise_product(einsum_form, coeffs[1], kernel[1])
    imag_part = precise_product(einsum_form, coeffs[0], kernel[1]) + precise_product(einsum_form, coeffs[1], kernel[0])
    return jnp.stack([real_part, imag_part])


def spectral_input_grad(d_mixed, kernel):
    einsum_form = "bolm,lio->bilm"
    real_part = precise_product(einsum_form, d_mixed[0], kernel[0]) + precise_product(einsum_form, d_mixed[1], kernel[1])
    imag_part = precise_product(einsum_form, d_mixed[1], kernel[0]) - precise_product(einsum_form, d_mixed[0], kernel[1])
    return jnp.stack([real_part, imag_part])


def spectral_kernel_grad(coeffs, d_mixed):
    einsum_form = "bilm,bolm->lio"
    real_part = precise_product(einsum_form, coeffs[0], d_mixed[0]) + precise_product(einsum_form, coeffs[1], d_mixed[1])
    imag_part = precise_product(einsum_form, coeffs[0], d_mixed[1]) - precise_product(einsum_form, coeffs[1], d_mixed[0])
    return jnp.stack([real_part, imag_part])


def solution(mesh):
    dp_size = mesh.shape["dp"]
    w_size = mesh.shape["w"]
    h_size = mesh.shape["h"]
    grid_axes = ("h", "w")
    all_axes = ("dp", "h", "w")

    def degree_from_lat(spec_loc, table):
        part_sums = precise_product("mlt,xbctm->xbclm", table, spec_loc)
        return lax.psum_scatter(part_sums, "h", scatter_dimension=3, tiled=True)

    def lat_from_degree(coeffs, table):
        coeffs_all = lax.all_gather(coeffs, "h", axis=3, tiled=True)
        return precise_product("mlt,xbclm->xbctm", table, coeffs_all)

    def local_step(field, target, lat_weight, leg_fwd, leg_inv, spec_w, w_in, w_out):
        batch_loc, chan_count, lat_loc, lon_loc = field.shape
        lon_count = lon_loc * w_size
        num_modes = leg_fwd.shape[0] * w_size
        grid_points = lat_loc * h_size * lon_count
        total_points = batch_loc * dp_size * chan_count * grid_points
        chan_mean = lax.psum(jnp.sum(field, axis=(2, 3), keepdims=True), grid_axes) / grid_points
        centred = field - chan_mean
        variance = lax.psum(jnp.sum(centred * centred, axis=(2, 3), keepdims=True), grid_axes) / grid_points
        inv_std = lax.rsqrt(variance + NORM_EPS)
        normed = centred * inv_std
        lon_whole = lax.all_to_all(normed, "w", 1, 3, tiled=True)
        spec_half, fwd_pull = jax.vjp(functools.partial(lon_forward, num_modes=num_modes), lon_whole)
        spec_loc = lax.all_to_all(spec_half, "w", 4, 2, tiled=True)
        coeffs = degree_from_lat(spec_loc, leg_fwd)
        mixed = spectral_mix(coeffs, spec_w)
        back_loc = lat_from_degree(mixed, leg_inv)
        back_half = lax.all_to_all(back_loc, "w", 2, 4, tiled=True)
        y_half, inv_pull = jax.vjp(functools.partial(lon_inverse, lon_count=lon_count), back_half)
        y_grid = lax.all_to_all(y_half, "w", 3, 1, tiled=True)
        y_bf = y_grid.astype(jnp.bfloat16)
        hidden = jnp.einsum("bctp,cf->bftp", y_bf, w_in, preferred_element_type=jnp.float32)
        activation, gelu_pull = jax.vjp(jax.nn.gelu, hidden)
        act_bf = activation.astype(jnp.bfloat16)
        mlp_out = jnp.einsum("bftp,fc->bctp", act_bf, w_out, preferred_element_type=jnp.float32)
        residual = field + y_grid + mlp_out - target
        d_out = lat_weight[None, None, :, None] * residual
        loss = lax.psum(jnp.sum(d_out * residual), all_axes) / total_points
        d_out_bf = d_out.astype(jnp.bfloat16)
        grad_w_out = lax.psum(jnp.einsum("bftp,bctp->fc", act_bf, d_out_bf, preferred_element_type=jnp.float32), all_axes)
        d_act = jnp.einsum("bctp,fc->bftp", d_out_bf, w_out, preferred_element_type=jnp.float32)
        d_hidden = gelu_pull(d_act)[0].astype(jnp.bfloat16)
        grad_w_in = lax.psum(jnp.einsum("bctp,bftp->cf", y_bf, d_hidden, preferred_element_type=jnp.float32), all_axes)
        d_y = d_out + jnp.einsum("bftp,cf->bctp", d_hidden, w_in, preferred_element_type=jnp.float32)
        d_y_half = lax.all_to_all(d_y, "w", 1, 3, tiled=True)
        d_back_half = inv_pull(d_y_half)[0]
        d_back_loc = lax.all_to_all(d_back_half, "w", 4, 2, tiled=True)
        d_mixed = degree_from_lat(d_back_loc, leg_inv)
        grad_spec = lax.psum(spectral_kernel_grad(coeffs, d_mixed), ("dp", "w"))
        d_coeffs = spectral_input_grad(d_mixed, spec_w)
        d_spec_loc = lat_from_degree(d_coeffs, leg_fwd)
        d_spec_half = lax.all_to_all(d_spec_loc, "w", 2, 4, tiled=True)
        d_lon_whole = fwd_pull(d_spec_half)[0]
        d_normed = lax.all_to_all(d_lon_whole, "w", 3, 1, tiled=True)
        norm_stats = lax.psum(jnp.stack([jnp.sum(d_normed, axis=(2, 3), keepdims=True), jnp.sum(d_normed * normed, axis=(2, 3), keepdims=True)]), grid_axes) / grid_points
        d_field = d_out + inv_std * (d_normed - norm_stats[0] - normed * norm_stats[1])
        return loss, d_field, grad_spec, grad_w_in, grad_w_out

    grid_spec = P("dp", None, "h", "w")
    table_spec = P("w", None, "h")
    kernel_spec = P(None, "h", None, None)
    return jax.shard_map(local_step, mesh=mesh, in_specs=(grid_spec, grid_spec, P("h"), table_spec, table_spec, kernel_spec, P(), P()), out_specs=(P(), grid_spec, kernel_spec, P(), P()), check_vma=False)
```

profile of v0, /device:TPU:1, one launch (start us, length us, event | category | flops | bytes accessed | tf_op | source)
XLA Modules:
  0.0 1326.1 jit_solution(9323936094311590689)
XLA Ops:
  10.0 65.1 %psum.42 = f32[12,32,1,1]{1,0,3,2:T(8,128)S(1)} all-reduce(f32[12,32,1,1]{1,0,3,2:T(8,128)S(1)} %bitcast.354), channel_id=1, replica_groups=mesh['dp'=8,'w'=4,'h'=8] {'h','w'}, use_global_device_ids=true, to_apply=%region_1.0 | all-reduce | flops 384 | bytes 3072 | tf_op jit(solution)/shard_map/psum | solution.py:68
  76.3 63.4 %psum.43 = f32[12,32,1,1]{1,0,3,2:T(8,128)S(1)} all-reduce(f32[12,32,1,1]{1,0,3,2:T(8,128)S(1)} %bitcast.355), channel_id=1, replica_groups=mesh['dp'=8,'w'=4,'h'=8] {'h','w'}, use_global_device_ids=true, to_apply=%region_3.0 | all-reduce | flops 384 | bytes 3072 | tf_op jit(solution)/shard_map/psum | solution.py:70
  157.5 11.3 all-to-all-done
  169.3 7.3 reduce.8
  200.0 7.0 copy.141
  212.4 12.4 all_to_all.121
  229.6 6.0 reshape.70
  235.6 6.9 copy.142
  242.5 6.8 copy.143
  249.3 13.2 convolution_bitcast_fusion.1
  262.5 12.9 copy.144
  282.3 72.9 %reduce-scatter.5.cloned.1.call-done = f32[2,12,32,8,16]{2,4,1,0,3:T(8,128)} async-done(((f32[2,12,32,64,16]{2,4,1,0,3:T(8,128)}), f32[2,12,32,8,16]{2,4,1,0,3:T(8,128)}) %reduce-scatter.5.cloned.1.call-update) | async-done | bytes 393232 | tf_op jit(solution)/shard_map/reduce_scatter | solution.py:56
  362.2 70.6 %all-gather.3.cloned.1.call-done = f32[2,12,32,64,16]{2,4,1,3,0:T(8,128)} async-done(((f32[2,12,32,8,16]{2,4,1,3,0:T(8,128)}), f32[2,12,32,64,16]{2,4,1,3,0:T(8,128)}) %all-gather.3.cloned.1.call-update) | async-done | bytes 3145744 | tf_op jit(solution)/shard_map/all_gather | solution.py:59
  432.8 18.4 %fusion.21 = f32[2,12,32,16,16]{2,3,1,0,4:T(8,128)} fusion(f32[2,12,32,64,16]{2,4,1,3,0:T(8,128)} %all-gather.3.cloned.1.call-done, f32[16,64,16]{1,2,0:T(8,128)S(1)} %copy-done), kind=kOutput, calls=%fused_computation.42 | convolution fusion | flops 150994944 | bytes 3997696 | tf_op jit(solution)/shard_map/mlt,xbclm->xbctm/dot_general | solution.py:12
  451.2 7.7 copy.149
  464.3 16.5 %all_to_all.122 = f32[4,1,49152]{2,1,0:T(1,128)} all-to-all(f32[4,1,49152]{2,1,0:T(1,128)} %reshape.71), channel_id=1, replica_groups=mesh['dp'=8,'w'=4,'h'=8] {'w'}, dimensions={0} | all-to-all | bytes 1572864 | tf_op jit(solution)/shard_map/all_to_all | solution.py:79
  485.5 6.0 reshape.72
  538.3 11.3 copy.153
  549.6 8.3 reshape.73
  557.9 24.2 %all_to_all.123 = f32[4,1,98304]{2,1,0:T(1,128)} all-to-all(f32[4,1,98304]{2,1,0:T(1,128)} %reshape.73), channel_id=1, replica_groups=mesh['dp'=8,'w'=4,'h'=8] {'w'}, dimensions={0} | all-to-all | bytes 3145728 | tf_op jit(solution)/shard_map/all_to_all | solution.py:81
  582.1 7.3 reduce.11
  589.4 10.5 reshape.74
  599.9 10.1 copy.154
  639.5 18.6 %all-to-all-done.4 = f32[4,1,98304]{2,1,0:T(1,128)} async-done(((f32[4,1,98304]{2,1,0:T(1,128)}), f32[4,1,98304]{2,1,0:T(1,128)}, u32[]{:S(2)}, u32[]{:S(2)}) %all-to-all-start.4) | async-done | bytes 1572896 | tf_op jit(solution)/shard_map/all_to_all | solution.py:96
  658.1 7.3 reduce.12
  689.0 7.0 copy.161
  701.4 13.7 %all_to_all.124 = f32[4,1,49152]{2,1,0:T(1,128)} all-to-all(f32[4,1,49152]{2,1,0:T(1,128)} %reshape.77), channel_id=1, replica_groups=mesh['dp'=8,'w'=4,'h'=8] {'w'}, dimensions={0} | all-to-all | bytes 1572864 | tf_op jit(solution)/shard_map/all_to_all | solution.py:98
  719.9 6.0 reshape.78
  725.9 6.9 copy.162
  732.8 6.7 copy.163
  739.5 13.2 convolution_bitcast_fusion
  752.7 12.9 copy.164
  765.7 76.5 %reduce-scatter.7.cloned.1.call-done = f32[2,12,32,8,16]{2,4,1,0,3:T(8,128)} async-done(((f32[2,12,32,64,16]{2,4,1,0,3:T(8,128)}), f32[2,12,32,8,16]{2,4,1,0,3:T(8,128)}) %reduce-scatter.7.cloned.1.call-update) | async-done | bytes 393232 | tf_op jit(solution)/shard_map/reduce_scatter | solution.py:56
  849.2 70.6 %all-gather.5.cloned.1.call-done = f32[2,12,32,64,16]{2,4,1,3,0:T(8,128)} async-done(((f32[2,12,32,8,16]{2,4,1,3,0:T(8,128)}), f32[2,12,32,64,16]{2,4,1,3,0:T(8,128)}) %all-gather.5.cloned.1.call-update) | async-done | bytes 3145744 | tf_op jit(solution)/shard_map/all_gather | solution.py:59
  919.8 18.4 %fusion.24 = f32[2,12,32,16,16]{2,3,1,0,4:T(8,128)} fusion(f32[2,12,32,64,16]{2,4,1,3,0:T(8,128)} %all-gather.5.cloned.1.call-done, f32[16,64,16]{1,2,0:T(8,128)S(1)} %copy-done.25), kind=kOutput, calls=%fused_computation.43 | convolution fusion | flops 150994944 | bytes 3997696 | tf_op jit(solution)/shard_map/mlt,xbclm->xbctm/dot_general | solution.py:12
  938.2 7.7 copy.168
  955.9 6.2 convolution_bitcast_fusion.6
  972.5 6.0 reshape.80
  1025.0 11.3 copy.172
  1036.3 8.3 reshape.81
  1059.5 8.8 all-to-all-done.7
  1068.3 7.3 reduce.15
  1075.6 10.9 reshape.82
  1086.5 10.4 copy.173
  1102.7 121.9 %psum.45 = f32[2,12,32,1,1]{2,0,4,3,1:T(2,128)S(1)} all-reduce(f32[2,12,32,1,1]{2,0,4,3,1:T(2,128)S(1)} %pad_maximum_fusion.16), channel_id=1, replica_groups=mesh['dp'=8,'w'=4,'h'=8] {'h','w'}, use_global_device_ids=true, to_apply=%region_10.11 | all-reduce | flops 768 | bytes 6144 | tf_op jit(solution)/shard_map/psum | solution.py:106
  1224.7 7.6 multiply_add_fusion
  1232.2 78.0 %all-reduce.13 = (f32[]{:T(128)}, f32[32,64]{1,0:T(8,128)}, f32[64,32]{0,1:T(8,128)}) all-reduce(f32[]{:T(128)} %get-tuple-element.47, f32[32,64]{1,0:T(8,128)S(1)} %convolution_bitcast_fusion.7, f32[64,32]{0,1:T(8,128)S(1)} %convolution_bitcast_fusion.6), channel_id=1, replica_groups=mesh['dp'=8,'w'=4,'h'=8] {'dp','h','w'}, use_global_device_ids=true, to_apply=%region_6.7 | all-reduce | flops 4097 | bytes 32776 | tf_op jit(solution)/shard_map/psum | solution.py:89
  1310.2 5.7 copy.180
  (189 shorter events, 285.1 us)
Async XLA Ops:
  7.2 425.6 %copy-start = (f32[16,64,16]{1,2,0:T(8,128)S(1)}, f32[16,64,16]{1,2,0:T(8,128)}, u32[]{:S(2)}) copy-start(f32[16,64,16]{1,2,0:T(8,128)} %param.15) | copy-start | bytes 196612
  7.2 68.0 %copy-start.1 = (f32[12,32,16,64]{3,2,1,0:T(8,128)S(1)}, f32[12,32,16,64]{3,2,1,0:T(8,128)}, u32[]{:S(2)}) copy-start(f32[12,32,16,64]{3,2,1,0:T(8,128)} %param.11) | copy-start | bytes 4718596
  75.2 65.7 %copy-start.26 = (f32[12,32]{1,0:T(8,128)}, f32[12,32]{1,0:T(8,128)S(1)}, u32[]{:S(2)}) copy-start(f32[12,32]{1,0:T(8,128)S(1)} %multiply_bitcast_fusion) | copy-start | bytes 4612
  139.8 1.1 copy-start.28
  149.2 19.6 %all-to-all-start = ((f32[4,1,98304]{2,1,0:T(1,128)}), f32[4,1,98304]{2,1,0:T(1,128)}, u32[]{:S(2)}, u32[]{:S(2)}) async-start(f32[4,1,98304]{2,1,0:T(1,128)} %reshape.67), calls=%async_computation | async-start | bytes 3145728 | tf_op jit(solution)/shard_map/all_to_all | solution.py:73
  153.5 201.7 %reduce-scatter.5.cloned.1.call-start = ((), (), s32[]{:S(2)}) async-start(), calls=%async_computation.10 | async-start | bytes 14155776 | tf_op jit(solution)/shard_map/reduce_scatter | solution.py:56
  191.4 4.0 copy-start.15
  191.4 6.4 copy-start.17
  242.5 6.8 copy-start.24
  275.4 0.7 copy-start.34
  275.4 157.4 %all-gather.3.cloned.1.call-start = ((), (), s32[]{:S(2)}) async-start(), calls=%async_computation.11 | async-start | bytes 14155776 | tf_op jit(solution)/shard_map/all_gather | solution.py:59
  355.2 4.0 copy-start.5
  504.8 5.0 copy-start.20
  526.4 5.6 copy-start.14
  527.7 6.8 copy-start.13
  527.7 6.8 copy-start.22
  599.9 10.1 copy-start.30
  610.0 3.1 copy-start.3
  610.0 3.8 copy-start.23
  610.0 3.8 copy-start.31
  613.8 4.2 copy-start.9
  613.8 4.2 copy-start.32
  618.0 5.6 copy-start.4
  623.6 3.1 copy-start.19
  635.1 23.0 %all-to-all-start.4 = ((f32[4,1,98304]{2,1,0:T(1,128)}), f32[4,1,98304]{2,1,0:T(1,128)}, u32[]{:S(2)}, u32[]{:S(2)}) async-start(f32[4,1,98304]{2,1,0:T(1,128)} %reshape.75), calls=%async_computation.5 | async-start | bytes 3145728 | tf_op jit(solution)/shard_map/all_to_all | solution.py:96
  639.4 202.7 %reduce-scatter.7.cloned.1.call-start = ((), (), s32[]{:S(2)}) async-start(), calls=%async_computation.12 | async-start | bytes 14155776 | tf_op jit(solution)/shard_map/reduce_scatter | solution.py:56
  680.3 4.0 copy-start.16
  680.3 6.4 copy-start.18
  686.7 0.7 slice-start
  765.6 154.1 %all-gather.5.cloned.1.call-start = ((), (), s32[]{:S(2)}) async-start(), calls=%async_computation.13 | async-start | bytes 14155776 | tf_op jit(solution)/shard_map/all_gather | solution.py:59
  842.1 4.0 copy-start.7
  847.0 72.8 %copy-start.25 = (f32[16,64,16]{1,2,0:T(8,128)S(1)}, f32[16,64,16]{1,2,0:T(8,128)}, u32[]{:S(2)}) copy-start(f32[16,64,16]{1,2,0:T(8,128)} %param.14) | copy-start | bytes 196612
  951.3 16.4 %all-to-all-start.6 = ((f32[4,1,49152]{2,1,0:T(1,128)}), f32[4,1,49152]{2,1,0:T(1,128)}, u32[]{:S(2)}, u32[]{:S(2)}) async-start(f32[4,1,49152]{2,1,0:T(1,128)} %reshape.79), calls=%async_computation.8 | async-start | bytes 1572864 | tf_op jit(solution)/shard_map/all_to_all | solution.py:103
  997.7 3.6 copy-start.33
  1004.4 1.2 copy-start.10
  1013.4 5.4 copy-start.11
  1013.4 5.4 copy-start.21
  1014.7 6.5 copy-start.12
  1044.6 23.6 %all-to-all-start.7 = ((f32[4,1,98304]{2,1,0:T(1,128)}), f32[4,1,98304]{2,1,0:T(1,128)}, u32[]{:S(2)}, u32[]{:S(2)}) async-start(f32[4,1,98304]{2,1,0:T(1,128)} %reshape.81), calls=%async_computation.9 | async-start | bytes 3145728 | tf_op jit(solution)/shard_map/all_to_all | solution.py:105
  1049.0 267.6 %all-reduce.16.cloned.1.call-start = ((), (), s32[]{:S(2)}) async-start(), calls=%async_computation.14 | async-start | bytes 524288 | tf_op jit(solution)/shard_map/psum | solution.py:100
  1049.2 3.7 copy-start.6
  1049.2 3.7 copy-start.8
  1096.8 2.8 copy-start.2
  1096.8 2.8 copy-start.27
  1096.8 2.8 copy-start.29
Sparse Core Ops, SparseCore 0:
  275.6 79.6 reduce-scatter.4
  362.3 70.4 all-gather.2
  765.7 76.3 reduce-scatter.6
  849.3 70.4 all-gather.4
  1059.6 145.3 all-reduce.15
where the time goes:
time: 1330 us
  blocking collectives  395 us (30%)
  waiting for transfers between devices  335 us (25%)
  local copies, waits for them, and re-layouts  333 us (25%)
  matrix products  143 us (11%)
  other arithmetic  84.6 us (6%)
  starting transfers between devices  18.4 us (1%)
  between operations  17.1 us (1%)
    reduce_scatter x2, waiting for transfers between devices, degree_from_lat(): return lax.psum_scatter(part_sums, 'h', scatter_dimension=3, tiled=True)  149 us
    all_gather x2, waiting for transfers between devices, lat_from_degree(): coeffs_all = lax.all_gather(coeffs, 'h', axis=3, tiled=True)  141 us
    psum x1, blocking collectives, local_step(): lax.psum(jnp.stack([jnp.sum(d_normed, axis=(2, 3), keepdims=True), jnp.su...  122 us
    unnamed x91, local copies, waits for them, and re-layouts  115 us
    dot_general x16, matrix products, precise_product(): jnp.einsum(einsum_form, operand_a, operand_b, precision=PRECISE, preferre...  80.2 us
    psum x1, blocking collectives, local_step(): loss = lax.psum(jnp.sum(d_out * residual), all_axes) / total_points  78 us
    psum x1, blocking collectives, local_step(): lax.psum(jnp.sum(field, axis=(2, 3), keepdims=True), grid_axes)  65.1 us
    psum x1, blocking collectives, local_step(): lax.psum(jnp.sum(centred * centred, axis=(2, 3), keepdims=True), grid_axes)  63.4 us
  transfers between devices with their start and end apart: 9, of which 8 were waited for; matrix products, arithmetic and copies ran while one was open for 6% of the time, Pallas kernels for 0%

commit v1 on v0

v1 whole, which is shorter than its diff:
```python
import functools
import numpy as np
import jax
import jax.numpy as jnp
from jax import lax
from jax.experimental import pallas as pl
from jax.experimental.pallas import tpu as pltpu
from jax.sharding import PartitionSpec as P

NORM_EPS = 1e-5
HI = lax.Precision.HIGHEST
GELU_C = 0.7978845608028654
GELU_A = 0.044715
NT = (((1,), (1,)), ((), ()))
NN = (((1,), (0,)), ((), ()))
F32 = jnp.float32
LANES, HALF_LANES, CHANS, ROWS = 128, 64, 32, 256
BF16 = jnp.bfloat16


def dot(a, b, dims, precision=HI):
    return lax.dot_general(a, b, dims, precision=precision, preferred_element_type=F32)


def dft_tables(nlon, modes, w_size, h_size):
    per = modes // (w_size * h_size)
    order = [w * (modes // w_size) + h * per + j for h in range(h_size) for w in range(w_size) for j in range(per)]
    m = np.array(order)[:, None]
    n = np.arange(nlon)[None, :]
    ang = 2.0 * np.pi * ((m * n) % nlon) / nlon
    fwd = np.concatenate([np.cos(ang), -np.sin(ang)]) / np.sqrt(nlon)
    mult = np.where(m == 0, 1.0, 2.0)
    inv = np.concatenate([mult * np.cos(ang), -mult * np.sin(ang)]) / np.sqrt(nlon)
    lon = nlon // w_size

    def spread(t):
        out = np.zeros((2, 2 * modes, w_size, 2, lon))
        for half in range(2):
            out[half, :, :, half, :] = t.reshape(2 * modes, w_size, lon)
        return out.reshape(4 * modes, 2 * nlon).astype(np.float32)

    return spread(fwd), spread(inv)

GROUPS = 3
MESH = pl.DeviceIdType.MESH


class Links:
    def __init__(self, send_sem, recv_sem):
        self.h, self.w, self.dp = lax.axis_index("h"), lax.axis_index("w"), lax.axis_index("dp")
        self.me = self.h * 4 + self.w
        self.send_sem, self.recv_sem = send_sem, recv_sem
        self.sent = []

    def plane_device(self, i):
        k = i + 1
        chip = lax.rem(5 * lax.rem(k, 16), 16)
        x = lax.rem(self.h // 2 + lax.rem(chip, 4), 4)
        w = lax.rem(self.w + chip // 4, 4)
        h = x * 2 + lax.rem(self.h + k // 16, 2)
        return h * 4 + w, {"h": h, "w": w}

    def axis_device(self, axis, n, i):
        t = lax.rem(getattr(self, axis) + 1 + i, n)
        return t, {axis: t}

    def greet(self):
        bar = pltpu.get_barrier_semaphore()

        def plane(i, c):
            pl.semaphore_signal(bar, inc=1, device_id=self.plane_device(i)[1], device_id_type=MESH)
            return c

        def depth(i, c):
            pl.semaphore_signal(bar, inc=1, device_id=self.axis_device("dp", 8, i)[1], device_id_type=MESH)
            return c

        lax.fori_loop(0, 31, plane, 0)
        lax.fori_loop(0, 7, depth, 0)
        pl.semaphore_wait(bar, 38)

    def start(self, src, dst, slot, dev):
        pltpu.make_async_remote_copy(
            src_ref=src, dst_ref=dst, send_sem=self.send_sem.at[slot], recv_sem=self.recv_sem.at[slot],
            device_id=dev, device_id_type=MESH).start()

    def plane_send(self, src, dst, g, rows, stage):
        mine = pl.ds(pl.multiple_of(self.me * rows, rows), rows)

        def one(i, c):
            t, dev = self.plane_device(i)
            theirs = pl.ds(pl.multiple_of(t * rows, rows), rows)
            self.start(src.at[g, theirs], dst.at[g, mine], stage * GROUPS + g, dev)
            return c

        lax.fori_loop(0, 31, one, 0)
        dst[g, mine, :] = src[g, mine, :]

    def plane_wait(self, dst, g, rows, stage, sem=None):
        part = dst.at[g, pl.ds(0, 31 * rows)]
        pltpu.make_async_copy(part, part, (self.recv_sem if sem is None else sem).at[stage * GROUPS + g]).wait()

    def axis_send(self, src_of, dst, axis, n, slot):
        def one(i, c):
            t, dev = self.axis_device(axis, n, i)
            self.start(src_of(t), dst.at[getattr(self, axis)], slot, dev)
            return c

        lax.fori_loop(0, n - 1, one, 0)

    def axis_wait(self, dst, n, slot, sem=None):
        part = dst.at[pl.ds(0, n - 1)]
        pltpu.make_async_copy(part, part, (self.recv_sem if sem is None else sem).at[slot]).wait()


def half_sums(row, low):
    a = jnp.sum(jnp.where(low, row, 0.0), axis=-1, keepdims=True)
    b = jnp.sum(jnp.where(low, 0.0, row), axis=-1, keepdims=True)
    return jnp.where(low, a, b)


def lane_low(shape):
    return lax.broadcasted_iota(jnp.int32, shape, len(shape) - 1) < HALF_LANES


def total(v):
    return jnp.sum(v.reshape(512, LANES), axis=0, keepdims=True)


def dft_stage(x_ref, g, m_ref, d_ref, st_ref):
    low = lane_low((1, LANES))
    v_all = x_ref[g].reshape(8, 4, 2, 16, LANES)
    cols = []
    for j in range(2):
        v = v_all[:, :, j]
        if st_ref is not None:
            mean = half_sums(total(v), low) * (1.0 / 32768.0)
            v = v - mean.reshape(1, 1, 1, LANES)
            var = half_sums(total(v * v), low) * (1.0 / 32768.0)
            inv = lax.rsqrt(var + NORM_EPS)
            v = v * inv.reshape(1, 1, 1, LANES)
            st_ref[g, j:j + 1, :] = mean
            st_ref[g, j + 4:j + 5, :] = inv
        cols.append(jnp.concatenate([v[:, w].reshape(LANES, LANES) for w in range(4)], axis=1))
    out = dot(m_ref[...], jnp.concatenate(cols, axis=0), NT)
    for half in range(2):
        for part in range(2):
            r0 = (half * 2 + part) * HALF_LANES
            for j in range(2):
                d_ref[g, pl.ds(part * 4 + j * 2 + half, HALF_LANES, stride=8), :] = out[r0:r0 + HALF_LANES, j * LANES:(j + 1) * LANES]


def idft_rows(z_ref, g, j, m_ref):
    parts = [z_ref[g, pl.ds(part * 4 + j * 2 + half, HALF_LANES, stride=8), :] for half in range(2) for part in range(2)]
    return dot(jnp.concatenate(parts, axis=0).T, m_ref[...], NN)


def join_grid(cols):
    per_j = [jnp.concatenate([c.reshape(8, 1, 16, LANES) for c in cols[j]], axis=1).reshape(8, 4, 1, 16, LANES) for j in range(2)]
    return jnp.concatenate(per_j, axis=2).reshape(1024, LANES)


def idft_stage(z_ref, g, m_ref, y_ref):
    cols = []
    for j in range(2):
        y = idft_rows(z_ref, g, j, m_ref)
        cols.append([y[:, w * LANES:(w + 1) * LANES] for w in range(4)])
    y_ref[g] = join_grid(cols)


def norm_back_stage(z_ref, g, m_ref, x_ref, st_ref, o_ref):
    low = lane_low((1, LANES))
    x_all = x_ref[g].reshape(8, 4, 2, 16, LANES)
    cols = []
    for j in range(2):
        y = idft_rows(z_ref, g, j, m_ref)
        mean, inv = st_ref[g, j:j + 1, :], st_ref[g, j + 4:j + 5, :]
        xs, ys, s0, s1 = [], [], 0.0, 0.0
        for w in range(4):
            yw = y[:, w * LANES:(w + 1) * LANES]
            xw = (x_all[:, w, j].reshape(LANES, LANES) - mean) * inv
            s0 = s0 + jnp.sum(yw, axis=0, keepdims=True)
            s1 = s1 + jnp.sum(yw * xw, axis=0, keepdims=True)
            xs.append(xw)
            ys.append(yw)
        s0 = half_sums(s0, low) * (1.0 / 32768.0)
        s1 = half_sums(s1, low) * (1.0 / 32768.0)
        cols.append([inv * (ys[w] - s0 - xs[w] * s1) for w in range(4)])
    o_ref[g] = join_grid(cols)


def swap_signed(t, top_sign):
    sub = lax.broadcasted_iota(jnp.int32, (8, LANES), 0)
    return jnp.where(sub < 4, top_sign, -top_sign) * pltpu.roll(t, 4, 0)


def to_degrees(x_ref, g, tab_ref):
    x = x_ref[g].reshape(CHANS, 2, 8, LANES)
    x = jnp.concatenate([x[:, 0].reshape(ROWS, LANES), x[:, 1].reshape(ROWS, LANES)], axis=1)
    return dot(x, tab_ref[...], NN)


def from_degrees(b, tab_ref, o_ref, g):
    y = dot(b, tab_ref[...], NT)
    y = jnp.concatenate([y[:, :LANES].reshape(CHANS, 1, 8, LANES), y[:, LANES:].reshape(CHANS, 1, 8, LANES)], axis=1)
    o_ref[g] = y.reshape(512, LANES)


def mix(src_ref, g, k_ref, dst_ref, adjoint):
    sign = 1.0 if adjoint else -1.0

    def body(c, acc):
        a = src_ref[g, pl.ds(pl.multiple_of(c * 8, 8), 8), :]
        s = swap_signed(a, sign)
        new = []
        for o in range(CHANS):
            if adjoint:
                kr, ki = k_ref[0, o, pl.ds(c, 1), :], k_ref[1, o, pl.ds(c, 1), :]
            else:
                kr, ki = k_ref[0, c, o:o + 1, :], k_ref[1, c, o:o + 1, :]
            new.append(acc[o] + (a * kr + s * ki))
        return tuple(new)

    acc = lax.fori_loop(0, CHANS, body, tuple(jnp.zeros((8, LANES), F32) for _ in range(CHANS)))
    for o in range(CHANS):
        dst_ref[o * 8:(o + 1) * 8, :] = acc[o]


def row_sums(v):
    sub = lax.broadcasted_iota(jnp.int32, (8, LANES), 0)
    low = sub < 4
    u = [jnp.where(low, v[j], v[j + 4]) + pltpu.roll(jnp.where(low, v[j + 4], v[j]), 4, 0) for j in range(4)]
    for step, n in ((2, 2), (1, 1)):
        first = lax.rem(sub // step, 2) == 0
        u = [jnp.where(first, u[j] + pltpu.roll(u[j], 8 - step, 0), u[j + n] + pltpu.roll(u[j + n], step, 0)) for j in range(n)]
    return u[0]


def kernel_grad(a_ref, d_ref, s_ref, gk_ref):
    def turn(o, carry):
        at = pl.ds(pl.multiple_of(o * 8, 8), 8)
        for g in range(GROUPS):
            s_ref[g, at, :] = swap_signed(d_ref[g, at, :], 1.0)
        return carry

    lax.fori_loop(0, CHANS, turn, 0)

    def rows(c, carry):
        at = pl.ds(pl.multiple_of(c * 8, 8), 8)
        a = [a_ref[g, at, :] for g in range(GROUPS)]
        for blk in range(4):
            for q, ref in ((0, d_ref), (1, s_ref)):
                prods = []
                for o in range(blk * 8, blk * 8 + 8):
                    prods.append(sum(a[g] * ref[g, o * 8:(o + 1) * 8, :] for g in range(GROUPS)))
                gk_ref[q, pl.ds(pl.multiple_of(c * CHANS + blk * 8, 8), 8), :] = row_sums(prods)
        return carry

    lax.fori_loop(0, CHANS, rows, 0)


def mlp_stage(y_ref, x_ref, t_ref, g, q, w1, w2, w1t, w2t, dy_ref, do_ref, sm_ref):
    for j in range(2):
        def take(ref):
            return jnp.concatenate([ref[g, pl.ds(j * 16 + r, CHANS, stride=CHANS), :] for r in range(16)], axis=1)

        y = take(y_ref)
        y_bf = y.astype(BF16)
        hid = dot(w1t, y_bf, NN, None)
        th = jnp.tanh(GELU_C * (hid + GELU_A * (hid * hid * hid)))
        cdf = 0.5 * (1.0 + th)
        act = (hid * cdf).astype(BF16)
        dgelu = cdf + (0.5 * hid * (1.0 - th * th)) * (GELU_C * (1.0 + (3.0 * GELU_A) * (hid * hid)))
        res = take(x_ref) + y + dot(w2t, act, NN, None) - take(t_ref)
        d_out = q * res
        sq = jnp.sum(d_out * res, axis=0, keepdims=True)
        sm_ref[CHANS:33, :] += sum(sq[:, r * LANES:(r + 1) * LANES] for r in range(16))
        d_bf = d_out.astype(BF16)
        g2 = dot(d_bf, act, NT, None)
        d_hid = (dot(w2, d_bf, NN, None) * dgelu).astype(BF16)
        g1 = dot(y_bf, d_hid, NT, None)
        sm_ref[0:CHANS, :] += jnp.concatenate([g1, g2], axis=1)
        d_y = d_out + dot(w1, d_hid, NN, None)
        for r in range(16):
            rows = pl.ds(j * 16 + r, CHANS, stride=CHANS)
            do_ref[g, rows, :] = d_out[:, r * LANES:(r + 1) * LANES]
            dy_ref[g, rows, :] = d_y[:, r * LANES:(r + 1) * LANES]


def pack_stage(x_ref, g, o_ref):
    parts = [jnp.concatenate([x_ref[g * 2 + j], x_ref[g * 2 + j + 6]], axis=-1) for j in range(2)]
    o_ref[g] = jnp.concatenate(parts, axis=1).reshape(1024, LANES)


BIG, HALF, SMALL = CHANS, 16, 40
EXTRA = 8 * GROUPS
(TAB, SM_A, SM_B, SM_C, GK_A, GK_B, GK_C) = range(EXTRA, EXTRA + 7)


def block_kernel(x_hbm, t_hbm, q_ref, w1_ref, w2t_ref, lp_ref, lq_ref, k_hbm, gf_hbm, gi_hbm,
                 out_hbm, gs_ref, smo_ref,
                 x_ref, t_ref, kw_ref, k_ref, gf_ref, gi_ref, q_row, tab,
                 s1, r1, s2, r2, s3, r3, s4, r4, s5, r5, s6, r6, s7, r7, s8, r8, tg, do,
                 st, acc_a, acc_d, acc_s, mixed, tabs, tp, tq, gk, gkt, gr1, gp, gr2, go, sm, sma, smb, smc, sb, sc,
                 send_sem, recv_sem, load_sem):
    links = Links(send_sem, recv_sem)
    low = lane_low((LANES, LANES))

    def load(src, dst, g, half):
        at = pl.ds(g * 2 + half * 6, 2)
        return pltpu.make_async_copy(src.at[at], dst.at[at], load_sem.at[(src is t_hbm) * 6 + g * 2 + half])

    for src, dst in ((x_hbm, x_ref), (t_hbm, t_ref)):
        for g in range(GROUPS):
            load(src, dst, g, 0).start()
            load(src, dst, g, 1).start()
        if src is x_hbm:
            tables = [pltpu.make_async_copy(a, b, load_sem.at[12 + i]) for i, (a, b) in enumerate(((gf_hbm, gf_ref), (k_hbm, kw_ref), (gi_hbm, gi_ref)))]
            for copy in tables:
                copy.start()
    links.greet()

    def groups(fn):
        def one(g, c):
            fn(g)
            return c

        lax.fori_loop(0, GROUPS, one, 0)

    def first(g):
        load(x_hbm, x_ref, g, 0).wait()
        load(x_hbm, x_ref, g, 1).wait()
        pack_stage(x_ref, g, s1)
        links.plane_send(s1, r1, g, BIG, 0)

    groups(first)
    for q, ref in ((0, lp_ref), (1, lq_ref)):
        for i in range(8):
            tab[i, q * 16:(q + 1) * 16, :] = jnp.concatenate([ref[2 * i], ref[2 * i + 1]], axis=1)
    links.axis_send(lambda t: tab.at[t], tabs, "h", 8, TAB)
    tabs[links.h] = tab[links.h]
    for r in range(16):
        q_row[:, r * LANES:(r + 1) * LANES] = jnp.full((1, LANES), q_ref[r], F32)
    for copy in tables:
        copy.wait()

    def widen(c, carry):
        for part in range(2):
            k_ref[part, c] = jnp.concatenate([kw_ref[part, c], kw_ref[part, c]], axis=1)
        return carry

    lax.fori_loop(0, CHANS, widen, 0)

    def take_target(g):
        load(t_hbm, t_ref, g, 0).wait()
        load(t_hbm, t_ref, g, 1).wait()
        pack_stage(t_ref, g, tg)

    groups(take_target)
    sm[...] = jnp.zeros((SMALL, LANES), F32)
    links.axis_wait(tabs, 8, TAB)
    for q, ref in ((0, tp), (1, tq)):
        rows = tabs[:, q * 16:(q + 1) * 16, :].reshape(LANES, LANES)
        ref[0:LANES, :] = jnp.where(low, rows, 0.0)
        ref[LANES:ROWS, :] = jnp.where(low, 0.0, rows)

    def second(g):
        links.plane_wait(r1, g, BIG, 0)
        dft_stage(r1, g, gf_ref, s2, st)
        links.plane_send(s2, r2, g, HALF, 1)

    def third(g):
        links.plane_wait(r2, g, HALF, 1)
        acc_a[g] = to_degrees(r2, g, tp)
        mix(acc_a, g, k_ref, mixed, False)
        from_degrees(mixed[...], tq, s3, g)
        links.plane_send(s3, r3, g, HALF, 2)

    def fourth(g):
        links.plane_wait(r3, g, HALF, 2)
        idft_stage(r3, g, gi_ref, s4)
        links.plane_send(s4, r4, g, BIG, 3)

    w1, w2t = w1_ref[...], w2t_ref[...]
    w1t, w2 = w1.astype(F32).T.astype(BF16), w2t.astype(F32).T.astype(BF16)

    def fifth(g):
        links.plane_wait(r4, g, BIG, 3)
        mlp_stage(r4, s1, tg, g, q_row[...], w1, w2, w1t, w2t, s5, do, sm)
        links.plane_send(s5, r5, g, BIG, 4)

    def sixth(g):
        links.plane_wait(r5, g, BIG, 4)
        dft_stage(r5, g, gi_ref, s6, None)
        links.plane_send(s6, r6, g, HALF, 5)

    def seventh(g):
        links.plane_wait(r6, g, HALF, 5)
        acc_d[g] = to_degrees(r6, g, tq)
        mix(acc_d, g, k_ref, mixed, True)
        from_degrees(mixed[...], tp, s7, g)
        links.plane_send(s7, r7, g, HALF, 6)

    def eighth(g):
        links.plane_wait(r7, g, HALF, 6)
        norm_back_stage(r7, g, gf_ref, r1, st, s8)
        links.plane_send(s8, r8, g, BIG, 7)

    def ninth(g):
        links.plane_wait(r8, g, BIG, 7)
        do[g] = do[g] + r8[g]
        pltpu.make_async_copy(do.at[g], out_hbm.at[g], load_sem.at[15 + g]).start()

    for stage in (second, third, fourth, fifth):
        groups(stage)

    links.axis_send(lambda t: sm, sma, "dp", 8, SM_A)
    sma[links.dp] = sm[...]
    groups(sixth)
    links.axis_wait(sma, 8, SM_A)
    sb[...] = jnp.sum(sma[...], axis=0)
    links.axis_send(lambda t: sb, smb, "h", 8, SM_B)
    smb[links.h] = sb[...]
    groups(seventh)
    links.axis_wait(smb, 8, SM_B)
    sc[...] = jnp.sum(smb[...], axis=0)
    links.axis_send(lambda t: sc, smc, "w", 4, SM_C)
    smc[links.w] = sc[...]


    kernel_grad(acc_a, acc_d, acc_s, gk)

    def turn(n, c):
        for q in range(2):
            t = gk[q, pl.ds(pl.multiple_of(n * LANES, LANES), LANES), :].T
            i = q * 8 + n
            gkt[i // 2, pl.ds(pl.multiple_of(lax.rem(i, 2) * HALF_LANES, HALF_LANES), HALF_LANES), :] = t[0:HALF_LANES] + t[HALF_LANES:LANES]
        return c

    lax.fori_loop(0, 8, turn, 0)
    links.axis_send(lambda t: gkt.at[t], gr1, "dp", 8, GK_A)
    gr1[links.dp] = gkt[links.dp]
    eighth(0)
    eighth(1)
    links.axis_wait(gr1, 8, GK_A)
    part = jnp.sum(gr1[...], axis=0)
    for n in range(2):
        gp[:, n * 8:(n + 1) * 8, :] = part[n * HALF_LANES:(n + 1) * HALF_LANES].reshape(8, 8, LANES)

    def spread(i, c):
        t, dev = links.plane_device(i)
        links.start(gp.at[t // 4], gr2.at[links.me], GK_B, dev)
        return c

    lax.fori_loop(0, 31, spread, 0)
    gr2[links.me] = gp[links.h]
    eighth(2)
    ninth(0)
    links.axis_wait(gr2, CHANS, GK_B)
    go[...] = jnp.sum(gr2[...], axis=0)
    links.axis_send(lambda t: go, gs_ref, "dp", 8, GK_C)
    gs_ref[links.dp] = go[...]
    links.axis_wait(smc, 4, SM_C)
    smo_ref[...] = jnp.sum(smc[...], axis=0)
    ninth(1)
    ninth(2)
    links.axis_wait(gs_ref, 8, GK_C)
    for g in range(GROUPS):
        pltpu.make_async_copy(do.at[g], out_hbm.at[g], load_sem.at[15 + g]).wait()

    for stage, (buf, rows) in enumerate(((s1, BIG), (s2, HALF), (s3, HALF), (s4, BIG), (s5, BIG), (s6, HALF), (s7, HALF), (s8, BIG))):
        groups(lambda g, buf=buf, rows=rows, stage=stage: links.plane_wait(buf, g, rows, stage, send_sem))
    for buf, n, slot in ((tabs, 8, TAB), (sma, 8, SM_A), (smb, 8, SM_B), (smc, 4, SM_C), (gr1, 8, GK_A), (gr2, CHANS, GK_B), (gs_ref, 8, GK_C)):
        links.axis_wait(buf, n, slot, send_sem)


def run_block(*args):
    big, half = pltpu.VMEM((GROUPS, 1024, LANES), F32), pltpu.VMEM((GROUPS, 512, LANES), F32)
    stages = [big, big, half, half, half, half, big, big, big, big, half, half, half, half, big, big, big, big]
    vm = lambda *s: pltpu.VMEM(s, F32)
    fields = [vm(12, CHANS, 16, HALF_LANES), vm(12, CHANS, 16, HALF_LANES), vm(2, CHANS, CHANS, HALF_LANES), vm(2, CHANS, CHANS, LANES), vm(ROWS, 512), vm(ROWS, 512), vm(1, 2048), vm(8, CHANS, LANES)]
    scratch = fields + stages + [
        vm(GROUPS, 8, LANES), vm(GROUPS, ROWS, LANES), vm(GROUPS, ROWS, LANES), vm(GROUPS, ROWS, LANES), vm(ROWS, LANES),
        vm(8, CHANS, LANES), vm(ROWS, LANES), vm(ROWS, LANES),
        vm(2, 1024, LANES), vm(8, LANES, LANES), vm(8, LANES, LANES), vm(8, 16, LANES), vm(CHANS, 16, LANES), vm(16, LANES),
        vm(SMALL, LANES), vm(8, SMALL, LANES), vm(8, SMALL, LANES), vm(4, SMALL, LANES), vm(SMALL, LANES), vm(SMALL, LANES),
        pltpu.SemaphoreType.DMA((EXTRA + 7,)), pltpu.SemaphoreType.DMA((EXTRA + 7,)), pltpu.SemaphoreType.DMA((18,)),
    ]
    space, hbm = pl.BlockSpec(memory_space=pltpu.VMEM), pl.BlockSpec(memory_space=pl.ANY)
    return pl.pallas_call(
        block_kernel,
        out_shape=[
            jax.ShapeDtypeStruct((GROUPS, 1024, LANES), F32),
            jax.ShapeDtypeStruct((8, 16, LANES), F32),
            jax.ShapeDtypeStruct((SMALL, LANES), F32),
        ],
        in_specs=[hbm, hbm, pl.BlockSpec(memory_space=pltpu.SMEM), space, space, space, space, hbm, hbm, hbm],
        out_specs=[hbm, space, space],
        scratch_shapes=scratch,
        compiler_params=pltpu.CompilerParams(collective_id=0, has_side_effects=True, vmem_limit_bytes=62 * 1024 * 1024),
        name="block",
    )(*args)


def unpack_kernel(v_ref, o_ref):
    for j in range(2):
        v = v_ref[0, :, j * 16:(j + 1) * 16, :]
        o_ref[0, j] = v[:, :, :HALF_LANES]
        o_ref[1, j] = v[:, :, HALF_LANES:]


def unpack(v):
    return pl.pallas_call(
        unpack_kernel,
        grid=(GROUPS,),
        in_specs=[pl.BlockSpec((1, CHANS, CHANS, LANES), lambda g: (g, 0, 0, 0))],
        out_specs=pl.BlockSpec((2, 2, CHANS, 16, HALF_LANES), lambda g: (0, g, 0, 0, 0)),
        out_shape=jax.ShapeDtypeStruct((2, 6, CHANS, 16, HALF_LANES), F32),
        name="unpack",
    )(v.reshape(GROUPS, CHANS, CHANS, LANES)).reshape(12, CHANS, 16, HALF_LANES)


def solution(mesh):
    w_size, h_size, dp_size = mesh.shape["w"], mesh.shape["h"], mesh.shape["dp"]
    fwd_np, inv_np = dft_tables(ROWS, HALF_LANES, w_size, h_size)

    def local_step(field, target, lat_weight, leg_fwd, leg_inv, spec_w, w_in, w_out):
        gf, gi = jnp.asarray(fwd_np), jnp.asarray(inv_np)
        packed, gs, sm = run_block(
            field, target, lat_weight, w_in, w_out.T, leg_fwd.transpose(0, 2, 1), leg_inv.transpose(0, 2, 1),
            spec_w.transpose(0, 2, 3, 1), gf, gi)
        d_field = unpack(packed)
        grad_spec = gs.reshape(2, 4, 2, 8, 4, CHANS).transpose(0, 3, 1, 2, 4, 5).reshape(2, 8, CHANS, CHANS)
        grad_w_in = sm[:CHANS, :HALF_LANES]
        grad_w_out = sm[:CHANS, HALF_LANES:].T
        loss = jnp.sum(sm[CHANS]) / (dp_size * 384 * 32768)
        return loss, d_field, grad_spec, grad_w_in, grad_w_out

    grid_spec = P("dp", None, "h", "w")
    table_spec = P("w", None, "h")
    kernel_out = P(None, "h", None, None)
    return jax.shard_map(local_step, mesh=mesh, in_specs=(grid_spec, grid_spec, P("h"), table_spec, table_spec, P(), P(), P()), out_specs=(P(), grid_spec, kernel_out, P(), P()), check_vma=False)
```

time: 1330 us -> 149 us (0.11)
  blocking collectives: 395 us -> 0 us
  waiting for transfers between devices: 335 us -> 0 us
  local copies, waits for them, and re-layouts: 333 us -> 1.62 us
  matrix products: 143 us -> 0 us
  Pallas kernels: 0 us -> 143 us
  other arithmetic: 84.6 us -> 1.35 us
  starting transfers between devices: 18.4 us -> 0 us
  between operations: 17.1 us -> 2.45 us
    psum x4 -> x0, blocking collectives: 328 us -> none  [the longest x1 122 us: local_step(): lax.psum(jnp.stack([jnp.sum(d_normed, axis=(2, 3), keepdims=True), jnp.su...]
    reduce_scatter x2 -> x0, waiting for transfers between devices: 149 us -> none  [degree_from_lat(): return lax.psum_scatter(part_sums, 'h', scatter_dimension=3, tiled=True)]
    pallas_call x0 -> x2, Pallas kernels: none -> 143 us  [the longest x1 139 us: run_block(): pl.pallas_call(block_kernel, out_shape=[jax.ShapeDtypeStruct((GROUPS, 102...]
    all_gather x2 -> x0, waiting for transfers between devices: 141 us -> none  [lat_from_degree(): coeffs_all = lax.all_gather(coeffs, 'h', axis=3, tiled=True)]
    unnamed x91 -> x4, local copies, waits for them, and re-layouts: 115 us -> 0.01 us
    dot_general x22 -> x0, matrix products: 106 us -> none  [the longest x16 80.2 us: precise_product(): jnp.einsum(einsum_form, operand_a, operand_b, precision=PRECISE, preferre...]
    all_to_all x4 -> x0, blocking collectives: 66.8 us -> none  [the longest x1 24.2 us: local_step(): y_grid = lax.all_to_all(y_half, 'w', 3, 1, tiled=True)]
    all_to_all x11 -> x0, local copies, waits for them, and re-layouts: 65.6 us -> none  [the longest x2 13.6 us: local_step(): spec_loc = lax.all_to_all(spec_half, 'w', 4, 2, tiled=True)]
  transfers between devices with their start and end apart: 9 -> 0, of which waited for: 8 -> 0; matrix products, arithmetic and copies ran while one was open for 6% -> 0% of each run, Pallas kernels for 0% -> 0%
where the time goes in v1:
time: 149 us
  Pallas kernels  143 us (96%)
  between operations  2.45 us (2%)
  local copies, waits for them, and re-layouts  1.62 us (1%)
    pallas_call x1, Pallas kernels, run_block(): pl.pallas_call(block_kernel, out_shape=[jax.ShapeDtypeStruct((GROUPS, 102...  139 us
    pallas_call x1, Pallas kernels, unpack(): pl.pallas_call(unpack_kernel, grid=(GROUPS,), in_specs=[pl.BlockSpec((1,...  3.87 us

profile of v1, /device:TPU:1, one launch (start us, length us, event | category | flops | bytes accessed | tf_op | source)
XLA Modules:
  0.0 148.6 jit_solution(15029720154947928045)
XLA Ops:
  0.6 139.3 %block.1 = (f32[3,1024,128]{2,1,0:T(8,128)}, f32[8,16,128]{2,1,0:T(8,128)}, f32[40,128]{1,0:T(8,128)}) custom-call(f32[12,32,16,64]{3,2,1,0:T(8,128)} %x_hbm.1, f32[12,32,16,64]{3,2,1,0:T(8,128)} %t_hbm.1, f32[16]{0:T(128)} %q_ref.1, bf16[32,64]{1,0:T(8,128)(2,1)} %w1_ref.1, bf16[32,64]{1,0:T(8,128)(2,1)} %bitcast.17, f32[16,16,64]{2,1,0:T(8,128)} %bitcast.15, ...), custom_call_target="tpu_custom_call" | custom-call | tf_op jit(solution)/shard_map/block/pallas_call | solution.py:490
  139.9 0.0 copy-start
  139.9 0.0 copy-start.1
  140.0 1.3 slice_reduce_fusion
  142.0 3.9 %unpack.1 = f32[2,6,32,16,64]{4,3,2,1,0:T(8,128)} custom-call(f32[3,32,32,128]{3,2,1,0:T(8,128)} %bitcast.11), custom_call_target="tpu_custom_call" | custom-call | tf_op jit(solution)/shard_map/unpack/pallas_call | solution.py:513
  145.8 0.0 copy-done
  145.8 0.2 reshape.24
  146.0 0.8 copy.15
  146.8 0.0 copy-done.1
  146.8 0.7 slice_bitcast_fusion
Async XLA Ops:
  139.9 5.9 %copy-start = (f32[8,16,128]{2,1,0:T(8,128)S(1)}, f32[8,16,128]{2,1,0:T(8,128)}, u32[]{:S(2)}) copy-start(f32[8,16,128]{2,1,0:T(8,128)} %get-tuple-element.10) | copy-start | bytes 196612
  139.9 6.8 %copy-start.1 = (f32[40,128]{1,0:T(8,128)S(1)}, f32[40,128]{1,0:T(8,128)}, u32[]{:S(2)}) copy-start(f32[40,128]{1,0:T(8,128)} %get-tuple-element.8) | copy-start | bytes 61444

commit v2 on v1

--- a/solution.py
+++ b/solution.py
@@ -45,19 +45,21 @@
 MESH = pl.DeviceIdType.MESH
 
 
+CHIPS = [int(d, 16) for d in "5af49e38d27c16b"]
+
+
 class Links:
     def __init__(self, send_sem, recv_sem):
         self.h, self.w, self.dp = lax.axis_index("h"), lax.axis_index("w"), lax.axis_index("dp")
         self.me = self.h * 4 + self.w
         self.send_sem, self.recv_sem = send_sem, recv_sem
-        self.sent = []
+        self.others = [self.plane_device(i) for i in range(31)]
 
     def plane_device(self, i):
-        k = i + 1
-        chip = lax.rem(5 * lax.rem(k, 16), 16)
-        x = lax.rem(self.h // 2 + lax.rem(chip, 4), 4)
+        chip, core = (CHIPS[i], 0) if i < 15 else ((0, *CHIPS)[i - 15], 1)
+        x = lax.rem(self.h // 2 + chip % 4, 4)
         w = lax.rem(self.w + chip // 4, 4)
-        h = x * 2 + lax.rem(self.h + k // 16, 2)
+        h = x * 2 + lax.rem(self.h + core, 2)
         return h * 4 + w, {"h": h, "w": w}
 
     def axis_device(self, axis, n, i):
@@ -67,15 +69,12 @@
     def greet(self):
         bar = pltpu.get_barrier_semaphore()
 
-        def plane(i, c):
-            pl.semaphore_signal(bar, inc=1, device_id=self.plane_device(i)[1], device_id_type=MESH)
-            return c
-
         def depth(i, c):
             pl.semaphore_signal(bar, inc=1, device_id=self.axis_device("dp", 8, i)[1], device_id_type=MESH)
             return c
 
-        lax.fori_loop(0, 31, plane, 0)
+        for _, dev in self.others:
+            pl.semaphore_signal(bar, inc=1, device_id=dev, device_id_type=MESH)
         lax.fori_loop(0, 7, depth, 0)
         pl.semaphore_wait(bar, 38)
 
@@ -87,13 +86,9 @@
     def plane_send(self, src, dst, g, rows, stage):
         mine = pl.ds(pl.multiple_of(self.me * rows, rows), rows)
 
-        def one(i, c):
-            t, dev = self.plane_device(i)
+        for t, dev in self.others:
             theirs = pl.ds(pl.multiple_of(t * rows, rows), rows)
             self.start(src.at[g, theirs], dst.at[g, mine], stage * GROUPS + g, dev)
-            return c
-
-        lax.fori_loop(0, 31, one, 0)
         dst[g, mine, :] = src[g, mine, :]
 
     def plane_wait(self, dst, g, rows, stage, sem=None):
@@ -404,7 +399,6 @@
     def eighth(g):
         links.plane_wait(r7, g, HALF, 6)
         norm_back_stage(r7, g, gf_ref, r1, st, s8)
-        links.plane_send(s8, r8, g, BIG, 7)
 
     def ninth(g):
         links.plane_wait(r8, g, BIG, 7)
@@ -440,28 +434,28 @@
     lax.fori_loop(0, 8, turn, 0)
     links.axis_send(lambda t: gkt.at[t], gr1, "dp", 8, GK_A)
     gr1[links.dp] = gkt[links.dp]
-    eighth(0)
-    eighth(1)
+    for g in range(2):
+        eighth(g)
+        links.plane_send(s8, r8, g, BIG, 7)
+    eighth(2)
     links.axis_wait(gr1, 8, GK_A)
     part = jnp.sum(gr1[...], axis=0)
     for n in range(2):
         gp[:, n * 8:(n + 1) * 8, :] = part[n * HALF_LANES:(n + 1) * HALF_LANES].reshape(8, 8, LANES)
 
-    def spread(i, c):
-        t, dev = links.plane_device(i)
+    for t, dev in links.others:
         links.start(gp.at[t // 4], gr2.at[links.me], GK_B, dev)
-        return c
-
-    lax.fori_loop(0, 31, spread, 0)
+    links.plane_send(s8, r8, 2, BIG, 7)
     gr2[links.me] = gp[links.h]
-    eighth(2)
     ninth(0)
     links.axis_wait(gr2, CHANS, GK_B)
     go[...] = jnp.sum(gr2[...], axis=0)
     links.axis_send(lambda t: go, gs_ref, "dp", 8, GK_C)
     gs_ref[links.dp] = go[...]
     links.axis_wait(smc, 4, SM_C)
-    smo_ref[...] = jnp.sum(smc[...], axis=0)
+    sums = jnp.sum(smc[...], axis=0)
+    smo_ref[0:CHANS, :] = sums[0:CHANS]
+    smo_ref[CHANS:40, :] = sums[CHANS:40] * (1.0 / 100663296.0)
     ninth(1)
     ninth(2)
     links.axis_wait(gs_ref, 8, GK_C)
@@ -502,22 +496,31 @@
     )(*args)
 
 
-def unpack_kernel(v_ref, o_ref):
+def unpack_kernel(v_ref, sm_ref, o_ref, g1_ref, g2_ref, loss_ref):
     for j in range(2):
         v = v_ref[0, :, j * 16:(j + 1) * 16, :]
         o_ref[0, j] = v[:, :, :HALF_LANES]
         o_ref[1, j] = v[:, :, HALF_LANES:]
 
-
-def unpack(v):
-    return pl.pallas_call(
+    @pl.when(pl.program_id(0) == 0)
+    def _():
+        g1_ref[...] = sm_ref[0:CHANS, 0:HALF_LANES]
+        g2_ref[...] = sm_ref[0:CHANS, HALF_LANES:LANES]
+        loss_ref[...] = jnp.sum(sm_ref[CHANS:33, :], axis=1, keepdims=True)
+
+
+def unpack(v, sm):
+    whole = lambda *shape: pl.BlockSpec(shape, lambda g: (0, 0))
+    out, g1, g2, loss = pl.pallas_call(
         unpack_kernel,
         grid=(GROUPS,),
-        in_specs=[pl.BlockSpec((1, CHANS, CHANS, LANES), lambda g: (g, 0, 0, 0))],
-        out_specs=pl.BlockSpec((2, 2, CHANS, 16, HALF_LANES), lambda g: (0, g, 0, 0, 0)),
-        out_shape=jax.ShapeDtypeStruct((2, 6, CHANS, 16, HALF_LANES), F32),
+        in_specs=[pl.BlockSpec((1, CHANS, CHANS, LANES), lambda g: (g, 0, 0, 0)), whole(SMALL, LANES)],
+        out_specs=[pl.BlockSpec((2, 2, CHANS, 16, HALF_LANES), lambda g: (0, g, 0, 0, 0)), whole(CHANS, HALF_LANES), whole(CHANS, HALF_LANES), whole(1, 1)],
+        out_shape=[jax.ShapeDtypeStruct((2, 6, CHANS, 16, HALF_LANES), F32), jax.ShapeDtypeStruct((CHANS, HALF_LANES), F32),
+                   jax.ShapeDtypeStruct((CHANS, HALF_LANES), F32), jax.ShapeDtypeStruct((1, 1), F32)],
         name="unpack",
-    )(v.reshape(GROUPS, CHANS, CHANS, LANES)).reshape(12, CHANS, 16, HALF_LANES)
+    )(v.reshape(GROUPS, CHANS, CHANS, LANES), sm)
+    return out.reshape(12, CHANS, 16, HALF_LANES), g1, g2.T, loss[0, 0]
 
 
 def solution(mesh):
@@ -529,11 +532,8 @@
         packed, gs, sm = run_block(
             field, target, lat_weight, w_in, w_out.T, leg_fwd.transpose(0, 2, 1), leg_inv.transpose(0, 2, 1),
             spec_w.transpose(0, 2, 3, 1), gf, gi)
-        d_field = unpack(packed)
+        d_field, grad_w_in, grad_w_out, loss = unpack(packed, sm)
         grad_spec = gs.reshape(2, 4, 2, 8, 4, CHANS).transpose(0, 3, 1, 2, 4, 5).reshape(2, 8, CHANS, CHANS)
-        grad_w_in = sm[:CHANS, :HALF_LANES]
-        grad_w_out = sm[:CHANS, HALF_LANES:].T
-        loss = jnp.sum(sm[CHANS]) / (dp_size * 384 * 32768)
         return loss, d_field, grad_spec, grad_w_in, grad_w_out
 
     grid_spec = P("dp", None, "h", "w")

time: 149 us -> 144 us (0.966)
  Pallas kernels: 143 us -> 141 us
  between operations: 2.45 us -> 0.65 us
    pallas_call x1, Pallas kernels: 139 us -> 137 us  [run_block(): pl.pallas_call(block_kernel, out_shape=[jax.ShapeDtypeStruct((GROUPS, 102...]
where the time goes in v2:
time: 144 us; the launch traced here: 143 us
  Pallas kernels  141 us (98%)
  local copies, waits for them, and re-layouts  1.77 us (1%)
    pallas_call x1, Pallas kernels, run_block(): pl.pallas_call(block_kernel, out_shape=[jax.ShapeDtypeStruct((GROUPS, 102...  137 us
    pallas_call x1, Pallas kernels, unpack(): pl.pallas_call(unpack_kernel, grid=(GROUPS,), in_specs=[pl.BlockSpec((1,...  3.87 us

profile of v2, /device:TPU:1, one launch (start us, length us, event | category | flops | bytes accessed | tf_op | source)
XLA Modules:
  0.0 143.2 jit_solution(16420312567226192846)
XLA Ops:
  0.6 136.9 %block.1 = (f32[3,1024,128]{2,1,0:T(8,128)}, f32[8,16,128]{2,1,0:T(8,128)}, f32[40,128]{1,0:T(8,128)}) custom-call(f32[12,32,16,64]{3,2,1,0:T(8,128)} %x_hbm.1, f32[12,32,16,64]{3,2,1,0:T(8,128)} %t_hbm.1, f32[16]{0:T(128)} %q_ref.1, bf16[32,64]{1,0:T(8,128)(2,1)} %w1_ref.1, bf16[32,64]{1,0:T(8,128)(2,1)} %bitcast.16, f32[16,16,64]{2,1,0:T(8,128)} %bitcast.14, ...), custom_call_target="tpu_custom_call" | custom-call | tf_op jit(solution)/shard_map/block/pallas_call | solution.py:484
  137.6 3.9 %unpack.1 = (f32[2,6,32,16,64]{4,3,2,1,0:T(8,128)}, f32[32,64]{1,0:T(8,128)}, f32[32,64]{1,0:T(8,128)}, f32[1,1]{1,0:T(1,128)}) custom-call(f32[3,32,32,128]{3,2,1,0:T(8,128)} %bitcast.10, f32[40,128]{1,0:T(8,128)} %get-tuple-element.13.sm_ref), custom_call_target="tpu_custom_call" | custom-call | tf_op jit(solution)/shard_map/unpack/pallas_call | solution.py:514
  141.4 1.0 reshape.24
  142.4 0.8 copy.15

commit v3 on v2

--- a/solution.py
+++ b/solution.py
@@ -353,12 +353,6 @@
 
     groups(take_target)
     sm[...] = jnp.zeros((SMALL, LANES), F32)
-    links.axis_wait(tabs, 8, TAB)
-    for q, ref in ((0, tp), (1, tq)):
-        rows = tabs[:, q * 16:(q + 1) * 16, :].reshape(LANES, LANES)
-        ref[0:LANES, :] = jnp.where(low, rows, 0.0)
-        ref[LANES:ROWS, :] = jnp.where(low, 0.0, rows)
-
     def second(g):
         links.plane_wait(r1, g, BIG, 0)
         dft_stage(r1, g, gf_ref, s2, st)
@@ -405,7 +399,13 @@
         do[g] = do[g] + r8[g]
         pltpu.make_async_copy(do.at[g], out_hbm.at[g], load_sem.at[15 + g]).start()
 
-    for stage in (second, third, fourth, fifth):
+    groups(second)
+    links.axis_wait(tabs, 8, TAB)
+    for q, ref in ((0, tp), (1, tq)):
+        rows = tabs[:, q * 16:(q + 1) * 16, :].reshape(LANES, LANES)
+        ref[0:LANES, :] = jnp.where(low, rows, 0.0)
+        ref[LANES:ROWS, :] = jnp.where(low, 0.0, rows)
+    for stage in (third, fourth, fifth):
         groups(stage)
 
     links.axis_send(lambda t: sm, sma, "dp", 8, SM_A)

time: 144 us -> 143 us (level)
  no operation moved by 1% of the time
where the time goes in v3:
time: 143 us
  Pallas kernels  140 us (98%)
  local copies, waits for them, and re-layouts  1.77 us (1%)
    pallas_call x1, Pallas kernels, run_block(): pl.pallas_call(block_kernel, out_shape=[jax.ShapeDtypeStruct((GROUPS, 102...  136 us
    pallas_call x1, Pallas kernels, unpack(): pl.pallas_call(unpack_kernel, grid=(GROUPS,), in_specs=[pl.BlockSpec((1,...  3.87 us

profile of v3, /device:TPU:1, one launch (start us, length us, event | category | flops | bytes accessed | tf_op | source)
XLA Modules:
  0.0 142.5 jit_solution(14221176496156646733)
XLA Ops:
  0.6 136.2 %block.1 = (f32[3,1024,128]{2,1,0:T(8,128)}, f32[8,16,128]{2,1,0:T(8,128)}, f32[40,128]{1,0:T(8,128)}) custom-call(f32[12,32,16,64]{3,2,1,0:T(8,128)} %x_hbm.1, f32[12,32,16,64]{3,2,1,0:T(8,128)} %t_hbm.1, f32[16]{0:T(128)} %q_ref.1, bf16[32,64]{1,0:T(8,128)(2,1)} %w1_ref.1, bf16[32,64]{1,0:T(8,128)(2,1)} %bitcast.16, f32[16,16,64]{2,1,0:T(8,128)} %bitcast.14, ...), custom_call_target="tpu_custom_call" | custom-call | tf_op jit(solution)/shard_map/block/pallas_call | solution.py:484
  136.9 3.9 %unpack.1 = (f32[2,6,32,16,64]{4,3,2,1,0:T(8,128)}, f32[32,64]{1,0:T(8,128)}, f32[32,64]{1,0:T(8,128)}, f32[1,1]{1,0:T(1,128)}) custom-call(f32[3,32,32,128]{3,2,1,0:T(8,128)} %bitcast.10, f32[40,128]{1,0:T(8,128)} %get-tuple-element.13.sm_ref), custom_call_target="tpu_custom_call" | custom-call | tf_op jit(solution)/shard_map/unpack/pallas_call | solution.py:514
  140.8 1.0 reshape.24
  141.8 0.8 copy.15
